TPU v7x, 32 devices: a whole 2x2x4 slice. The times are simulated.
32 devices in a mesh: row: 4 (over x, core), col: 8 (over z, y).
Axes of the slice: x: 2, y: 2, z: 4, core: 2. Of those that a mesh axis runs over, the one named last changes fastest.
Arguments:
- w_rec: bfloat16 [2, 4096, 4, 4096], P(None, 'row', None, 'col'), may hold values from -0.09375 to 0.09375
- w_in: bfloat16 [2, 4096, 4, 4096], P(None, 'row', None, 'col'), may hold values from -0.09375 to 0.09375
- gate_pre: float32 [2, 6, 64, 4, 4096], P(None, None, None, None, 'col'), may hold values from -8 to 8, as said below
- cells: float32 [2, 7, 64, 4096], P(None, None, None, 'col'), may hold values from -6 to 6
- layer_in: bfloat16 [2, 6, 64, 4096], P(None, None, None, 'row'), may hold values from -1 to 1
- h_prev: bfloat16 [2, 6, 64, 4096], P(None, None, None, 'row'), may hold values from -1 to 1
- top_grad: float32 [6, 64, 4096], P(None, None, 'col'), may hold values from -40 to 40
Outputs:
- w_rec_grad: bfloat16 [2, 4096, 4, 4096], P(None, 'row', None, 'col')
- w_in_grad: bfloat16 [2, 4096, 4, 4096], P(None, 'row', None, 'col')
- input_grad: float32 [6, 64, 4096], P(None, None, 'col')
Inputs may be any that keep to these rules, and one draw needn't show every extreme that they name: `gate_pre`: dimension 3 holds the input, forget, candidate and output gates in that order.
All inputs are finite; a program needn't handle non-finite values.
Results may differ from a plain program's by a relative error of at most 0.0051.
Values sent between devices are 32-bit elements; how exact they have to be, the bound alone decides.
A program may use at most 128 MiB of HBM per device.

v0:
```python
import functools

import jax
import jax.numpy as jnp
from jax import lax
from jax.experimental import pallas as pl
from jax.experimental.pallas import tpu as pltpu
from jax.sharding import PartitionSpec as P

MESH = pl.DeviceIdType.MESH


def split_col(cols, ratio):
    fast = 1
    while fast * fast * 2 <= cols:
        fast *= 2
    while fast < ratio:
        fast *= 2
    return cols // fast, fast


def exchange_kernel(blocks, rows, cols, scalar, *refs):
    ratio = cols // rows
    slow_n, fast_n = split_col(cols, ratio)
    per = fast_n // ratio
    parts, refs = refs[:blocks], refs[blocks:]
    if scalar:
        sq_in, out, sq_out = refs[:3]
        refs = refs[3:]
    else:
        out = refs[0]
        refs = refs[1:]
    recv1, acc1, recv2, acc2, land, s1, r1, s2, r2, s3, r3 = refs[:11]
    if scalar:
        sq1, sqa1, sq2, sqa2, sq3, qs1, qr1, qs2, qr2, qs3, qr3 = refs[11:]
    width = recv1.shape[-1]
    mini = acc2.shape[1]
    row = lax.axis_index("row")
    col = lax.axis_index("col")
    slow, fast = col // fast_n, col % fast_n
    target = ratio * row + fast // per
    is_own = target == col
    source_row = col // ratio

    def fast_peer(d):
        return slow * fast_n + (fast + d) % fast_n

    def slow_peer(d):
        return ((slow + d) % slow_n) * fast_n + fast

    def source_col(z, j):
        return z * fast_n + (col % ratio) * per + j

    barrier = pltpu.get_barrier_semaphore()

    def greet(device):
        pl.semaphore_signal(barrier, inc=1, device_id=device, device_id_type=MESH)

    for d in range(1, fast_n):
        greet((row, fast_peer(d)))
    for d in range(1, slow_n):
        greet((row, slow_peer(d)))
    for z in range(slow_n):
        for j in range(per):
            other = source_col(z, j)

            @pl.when(jnp.logical_not((source_row == row) & (other == col)))
            def _(other=other):
                greet((source_row, other))

    count = fast_n - 1 + slow_n - 1 + rows - 1
    if scalar:
        for d in range(1, rows):
            greet(((row + d) % rows, col))
        count += rows - 1
    pl.semaphore_wait(barrier, count + jnp.where(is_own, 0, 1))

    def lanes(index):
        return pl.ds(pl.multiple_of(index * width, width), width)

    def subs(index):
        return pl.ds(pl.multiple_of(index * mini, mini), mini)

    def remote(src, dst, send, recv, device):
        return pltpu.make_async_remote_copy(
            src_ref=src, dst_ref=dst, send_sem=send, recv_sem=recv,
            device_id=device, device_id_type=MESH,
        )

    def copy1(b, d):
        peer = (fast + d) % fast_n
        return remote(parts[b].at[:, lanes(peer)], recv1.at[b, d - 1], s1.at[b, d - 1],
                      r1.at[b, d - 1], (row, fast_peer(d)))

    def copy2(b, d):
        peer = (slow + d) % slow_n
        return remote(acc1.at[b, subs(peer), :], recv2.at[b, d - 1], s2.at[b, d - 1],
                      r2.at[b, d - 1], (row, slow_peer(d)))

    def copy3(b, d):
        return remote(acc2.at[b], land.at[b, subs(slow), lanes(fast % per)], s3.at[b, d],
                      r3.at[b, slow * per + fast % per], ((row + d) % rows, target))

    def scalar1(d):
        return remote(sq_in, sq1.at[d - 1], qs1.at[d - 1], qr1.at[d - 1], (row, fast_peer(d)))

    def scalar2(d):
        return remote(sqa1, sq2.at[d - 1], qs2.at[d - 1], qr2.at[d - 1], (row, slow_peer(d)))

    def scalar3(d):
        return remote(sqa2, sq3.at[d - 1], qs3.at[d - 1], qr3.at[d - 1], ((row + d) % rows, col))

    if scalar:
        for d in range(1, fast_n):
            scalar1(d).start()
    for b in range(blocks):
        for d in range(1, fast_n):
            copy1(b, d).start()
    if scalar:
        value = sq_in[...]
        for d in range(1, fast_n):
            scalar1(d).wait_recv()
            value = value + sq1[d - 1]
        sqa1[...] = value
        for d in range(1, slow_n):
            scalar2(d).start()
    for b in range(blocks):
        value = parts[b][:, lanes(fast)]
        for d in range(1, fast_n):
            copy1(b, d).wait_recv()
            value = value + recv1[b, d - 1]
        acc1[b] = value
        for d in range(1, slow_n):
            copy2(b, d).start()
    if scalar:
        value = sqa1[...]
        for d in range(1, slow_n):
            scalar2(d).wait_recv()
            value = value + sq2[d - 1]
        sqa2[...] = value
        for d in range(1, rows):
            scalar3(d).start()
    for b in range(blocks):
        value = acc1[b, subs(slow), :]
        for d in range(1, slow_n):
            copy2(b, d).wait_recv()
            value = value + recv2[b, d - 1]
        acc2[b] = value

        @pl.when(is_own)
        def _(b=b, value=value):
            land[b, subs(slow), lanes(fast % per)] = value

        @pl.when(jnp.logical_not(is_own))
        def _(b=b):
            copy3(b, 0).start()

        for d in range(1, rows):
            copy3(b, d).start()
    if scalar:
        value = sqa2[...]
        for d in range(1, rows):
            scalar3(d).wait_recv()
            value = value + sq3[d - 1]
        sq_out[...] = value
    for b in range(blocks):
        for z in range(slow_n):
            for j in range(per):
                mine = (source_row == row) & (source_col(z, j) == col)

                @pl.when(jnp.logical_not(mine))
                def _(b=b, z=z, j=j):
                    spot = land.at[b, pl.ds(z * mini, mini), pl.ds(j * width, width)]
                    remote(spot, spot, s3.at[b, 0], r3.at[b, z * per + j],
                           (source_row, source_col(z, j))).wait_recv()

        out[b] = land[b]
    for b in range(blocks):
        for d in range(1, fast_n):
            copy1(b, d).wait_send()
        for d in range(1, slow_n):
            copy2(b, d).wait_send()
        for d in range(1, rows):
            copy3(b, d).wait_send()

        @pl.when(jnp.logical_not(is_own))
        def _(b=b):
            copy3(b, 0).wait_send()
    if scalar:
        for d in range(1, fast_n):
            scalar1(d).wait_send()
        for d in range(1, slow_n):
            scalar2(d).wait_send()
        for d in range(1, rows):
            scalar3(d).wait_send()


def exchange(parts, squares, collective):
    rows, cols = lax.axis_size("row"), lax.axis_size("col")
    ratio = cols // rows
    slow_n, fast_n = split_col(cols, ratio)
    blocks = len(parts)
    batch, units = parts[0].shape
    width, mini = units // fast_n, batch // slow_n
    scalar = squares is not None
    per = fast_n // ratio
    dma = pltpu.SemaphoreType.DMA
    vmem = lambda *shape: pltpu.VMEM(shape, jnp.float32)
    scratch = [
        vmem(blocks, fast_n - 1, batch, width), vmem(blocks, batch, width),
        vmem(blocks, slow_n - 1, mini, width), vmem(blocks, mini, width),
        vmem(blocks, batch, units // ratio),
        dma((blocks, fast_n - 1)), dma((blocks, fast_n - 1)),
        dma((blocks, slow_n - 1)), dma((blocks, slow_n - 1)),
        dma((blocks, rows)), dma((blocks, slow_n * per)),
    ]
    shapes = [jax.ShapeDtypeStruct((blocks, batch, units // ratio), jnp.float32)]
    args = list(parts)
    if scalar:
        args.append(squares)
        shapes.append(jax.ShapeDtypeStruct(squares.shape, jnp.float32))
        tile = squares.shape
        scratch += [
            vmem(fast_n - 1, *tile), vmem(*tile), vmem(slow_n - 1, *tile), vmem(*tile), vmem(rows - 1, *tile),
            dma((fast_n - 1,)), dma((fast_n - 1,)), dma((slow_n - 1,)), dma((slow_n - 1,)),
            dma((rows - 1,)), dma((rows - 1,)),
        ]
    in_vmem = pl.BlockSpec(memory_space=pltpu.VMEM)
    return pl.pallas_call(
        functools.partial(exchange_kernel, blocks, rows, cols, scalar),
        out_shape=shapes,
        in_specs=[in_vmem] * len(args),
        out_specs=[in_vmem] * len(shapes),
        scratch_shapes=scratch,
        compiler_params=pltpu.CompilerParams(collective_id=collective, has_side_effects=True),
        name="exchange",
    )(*args)


def cell_backward(preact, cell_prev, cell_now, hid_grad, cell_carry):
    in_gate = jax.nn.sigmoid(preact[:, 0])
    forget = jax.nn.sigmoid(preact[:, 1])
    cand_gate = jnp.tanh(preact[:, 2])
    out_gate = jax.nn.sigmoid(preact[:, 3])
    tanh_cell = jnp.tanh(cell_now)
    cell_grad = cell_carry + hid_grad * out_gate * (1.0 - tanh_cell * tanh_cell)
    grad_in = cell_grad * cand_gate * in_gate * (1.0 - in_gate)
    grad_forget = cell_grad * cell_prev * forget * (1.0 - forget)
    grad_cand = cell_grad * in_gate * (1.0 - cand_gate * cand_gate)
    grad_out = hid_grad * tanh_cell * out_gate * (1.0 - out_gate)
    gates = jnp.concatenate([grad_in, grad_forget, grad_cand, grad_out], axis=1)
    return (gates.astype(jnp.bfloat16), cell_grad * forget)


def contract(left, right, dims):
    return lax.dot_general(left, right, ((dims, dims), ((), ())), preferred_element_type=jnp.float32)


def local(w_rec, w_in, gate_pre, cells, layer_in, h_prev, top_grad):
    layers, row_units = w_rec.shape[:2]
    steps, batch, col_units = top_grad.shape
    rec_flats = [w_rec[layer].reshape(row_units, 4 * col_units) for layer in range(layers)]
    in_flats = [w_in[layer].reshape(row_units, 4 * col_units) for layer in range(layers)]
    zeros = jnp.zeros((batch, col_units), jnp.float32)
    recurrent = [zeros] * layers
    carry = [zeros] * layers
    incoming = [None] * layers
    store = [[None] * steps for _ in range(layers)]
    for diagonal in range(steps + layers - 1):
        parts, goes = [], []
        for layer in range(layers - 1, -1, -1):
            step = steps - 1 - diagonal + layers - 1 - layer
            if not 0 <= step < steps:
                continue
            outside = top_grad[step] if layer == layers - 1 else incoming[layer]
            gates, carry[layer] = cell_backward(
                gate_pre[layer, step], cells[layer, step], cells[layer, step + 1],
                outside + recurrent[layer], carry[layer],
            )
            store[layer][step] = gates
            if step > 0:
                parts.append(contract(gates, rec_flats[layer], (1,)))
                goes.append((recurrent, layer))
            if layer > 0:
                parts.append(contract(gates, in_flats[layer], (1,)))
                goes.append((incoming, layer - 1))
        if parts:
            units = exchange(parts, None, len(parts))[0]
            for index, (where, layer) in enumerate(goes):
                where[layer] = units[index]
    flats = [jnp.concatenate(store[layer], axis=0) for layer in range(layers)]
    rec_in = [h_prev[layer].reshape(steps * batch, row_units) for layer in range(layers)]
    lay_in = [layer_in[layer].reshape(steps * batch, row_units) for layer in range(layers)]
    sumsq = 0.0
    for layer in range(layers):
        inputs_gram = contract(rec_in[layer], rec_in[layer], (1,)) + contract(lay_in[layer], lay_in[layer], (1,))
        sumsq = sumsq + jnp.sum(inputs_gram * contract(flats[layer], flats[layer], (1,)))
    last = [contract(store[0][step], in_flats[0], (1,)) for step in range(steps)]
    input_grad, squares = exchange(last, jnp.broadcast_to(sumsq, (8, 128)), 0)
    entries = 2.0 * layers * (row_units * lax.axis_size("row")) * (4 * col_units * lax.axis_size("col"))
    scale = 1.0 / jnp.maximum(jnp.sqrt(squares[0, 0] / entries), 0.05)

    def weight_grad(inputs):
        return jnp.stack([
            (contract(inputs[layer], flats[layer], (0,)) * scale).astype(jnp.bfloat16)
            .reshape(row_units, 4, col_units)
            for layer in range(layers)
        ])

    return (weight_grad(rec_in), weight_grad(lay_in), input_grad)


def solution(mesh):
    placed = (
        P(None, "row", None, "col"),
        P(None, "row", None, "col"),
        P(None, None, None, None, "col"),
        P(None, None, None, "col"),
        P(None, None, None, "row"),
        P(None, None, None, "row"),
        P(None, None, "col"),
    )
    return jax.shard_map(
        local,
        mesh=mesh,
        in_specs=placed,
        out_specs=(P(None, "row", None, "col"), P(None, "row", None, "col"), P(None, None, "col")),
        check_vma=False,
    )
```

profile of v0, /device:TPU:0, one launch (start us, length us, event | category | flops | bytes accessed | tf_op | source)
XLA Modules:
  0.0 445.5 jit_solution(8062317137677841627)
XLA Ops:
  0.7 5.6 %fusion.294 = (f32[1,1,64,4,512]{4,3,2,1,0:T(4,128)}, f32[1,1,64,4,512]{4,3,2,1,0:T(4,128)}, f32[1,1,64,4,512]{4,3,2,1,0:T(4,128)}, f32[1,1,64,4,512]{4,3,2,1,0:...) fusion(f32[2,6,64,4,512]{4,3,2,1,0:T(4,128)} %param.9), kind=kLoop, calls=%fused_computation.458 | loop fusion | bytes 12582912 | tf_op jit(solution)/shard_map/slice | solution.py:277
  8.5 4.2 fusion.292
  16.3 4.1 fusion.293
  26.0 28.0 %exchange.7 = f32[2,64,512]{2,1,0:T(8,128)} custom-call(f32[64,1024]{1,0:T(8,128)} %fusion.279.refs_0_, f32[64,1024]{1,0:T(8,128)} %fusion.278.refs_1_), custom_call_target="tpu_custom_call" | custom-call | tf_op jit(solution)/shard_map/exchange/pallas_call | solution.py:229
  55.3 2.4 copy_bitcast_fusion.8
  68.5 36.3 %exchange.8 = f32[3,64,512]{2,1,0:T(8,128)} custom-call(f32[64,1024]{1,0:T(8,128)} %fusion.277.refs_0_, f32[64,1024]{1,0:T(8,128)} %fusion.276.refs_1_, f32[64,1024]{1,0:T(8,128)} %fusion.275.refs_2_), custom_call_target="tpu_custom_call" | custom-call | tf_op jit(solution)/shard_map/exchange/pallas_call | solution.py:229
  106.3 2.5 copy_bitcast_fusion.6
  116.5 33.6 %exchange.9 = f32[3,64,512]{2,1,0:T(8,128)} custom-call(f32[64,1024]{1,0:T(8,128)} %fusion.273.refs_0_, f32[64,1024]{1,0:T(8,128)} %fusion.272.refs_1_, f32[64,1024]{1,0:T(8,128)} %fusion.271.refs_2_), custom_call_target="tpu_custom_call" | custom-call | tf_op jit(solution)/shard_map/exchange/pallas_call | solution.py:229
  161.2 37.1 %exchange.10 = f32[3,64,512]{2,1,0:T(8,128)} custom-call(f32[64,1024]{1,0:T(8,128)} %fusion.269.refs_0_, f32[64,1024]{1,0:T(8,128)} %fusion.268.refs_1_, f32[64,1024]{1,0:T(8,128)} %fusion.267.refs_2_), custom_call_target="tpu_custom_call" | custom-call | tf_op jit(solution)/shard_map/exchange/pallas_call | solution.py:229
  209.3 33.7 %exchange.11 = f32[3,64,512]{2,1,0:T(8,128)} custom-call(f32[64,1024]{1,0:T(8,128)} %fusion.265.refs_0_, f32[64,1024]{1,0:T(8,128)} %fusion.264.refs_1_, f32[64,1024]{1,0:T(8,128)} %fusion.263.refs_2_), custom_call_target="tpu_custom_call" | custom-call | tf_op jit(solution)/shard_map/exchange/pallas_call | solution.py:229
  244.5 2.5 copy_bitcast_fusion
  253.3 26.3 %exchange.12 = f32[2,64,512]{2,1,0:T(8,128)} custom-call(f32[64,1024]{1,0:T(8,128)} %fusion.257.refs_0_, f32[64,1024]{1,0:T(8,128)} %fusion.261.refs_1_), custom_call_target="tpu_custom_call" | custom-call | tf_op jit(solution)/shard_map/exchange/pallas_call | solution.py:229
  292.8 3.6 copy.41
  309.3 63.7 %exchange.13 = (f32[6,64,512]{2,1,0:T(8,128)}, f32[8,128]{1,0:T(8,128)}) custom-call(f32[64,1024]{1,0:T(8,128)} %fusion.254.refs_0_, f32[64,1024]{1,0:T(8,128)} %fusion.260.refs_1_, f32[64,1024]{1,0:T(8,128)} %fusion.262.refs_2_, f32[64,1024]{1,0:T(8,128)} %fusion.266.refs_3_, f32[64,1024]{1,0:T(8,128)} %fusion.270.refs_4_, f32[64,1024]{1,0:T(8,128)} %fusion.274.refs_5_, ...), custom_call_target="tpu_custom_call" | custom-call | tf_op jit(solution)/shard_map/exchange/pallas_call | solution.py:229
  374.9 5.8 %multiply_convert_fusion.1 = bf16[2048,1024]{1,0:T(8,128)(2,1)} fusion(bf16[384,2048]{1,0:T(8,128)(2,1)} %copy-done.141, bf16[384,1024]{1,0:T(8,128)(2,1)S(1)} %bitcast.772, f32[]{:T(128)} %bitcast.90), kind=kOutput, calls=%fused_computation.3 | convolution fusion | flops 1614807040 | bytes 6553604 | tf_op jit(solution)/shard_map/dot_general | solution.py:256
  380.8 7.9 %copy.24 = bf16[1,1024,4,512]{3,2,1,0:T(4,128)(2,1)} copy(bf16[1,1024,4,512]{1,3,2,0:T(8,128)(2,1)} %bitcast.775) | data formatting | bytes 8388608 | tf_op jit(solution)/shard_map/stack;reshape | solution.py:304
  388.6 5.8 %multiply_convert_fusion = bf16[2048,1024]{1,0:T(8,128)(2,1)} fusion(bf16[384,2048]{1,0:T(8,128)(2,1)} %copy-done.139, bf16[384,1024]{1,0:T(8,128)(2,1)S(1)} %bitcast.770, f32[]{:T(128)} %bitcast.90), kind=kOutput, calls=%fused_computation.2 | convolution fusion | flops 1614807040 | bytes 6553604 | tf_op jit(solution)/shard_map/dot_general | solution.py:256
  394.4 7.8 %copy.25 = bf16[1,1024,4,512]{3,2,1,0:T(4,128)(2,1)} copy(bf16[1,1024,4,512]{1,3,2,0:T(8,128)(2,1)} %bitcast.776) | data formatting | bytes 8388608 | tf_op jit(solution)/shard_map/stack;reshape | solution.py:304
  402.3 8.8 %pad_maximum_fusion.1 = bf16[2,1024,4,512]{3,2,1,0:T(4,128)(2,1)} fusion(bf16[1,1024,4,512]{3,2,1,0:T(4,128)(2,1)} %copy.25, bf16[1,1024,4,512]{3,2,1,0:T(4,128)(2,1)} %copy.24), kind=kLoop, calls=%fused_computation.1 | loop fusion | flops 4194304 | bytes 16777216 | tf_op jit(solution)/shard_map/stack | solution.py:304
  411.0 4.4 multiply_convert_fusion.3
  415.5 8.0 %copy.22 = bf16[1,1024,4,512]{3,2,1,0:T(4,128)(2,1)} copy(bf16[1,1024,4,512]{1,3,2,0:T(8,128)(2,1)} %bitcast.774) | data formatting | bytes 8388608 | tf_op jit(solution)/shard_map/stack;reshape | solution.py:304
  423.4 4.4 multiply_convert_fusion.2
  427.8 7.9 %copy.23 = bf16[1,1024,4,512]{3,2,1,0:T(4,128)(2,1)} copy(bf16[1,1024,4,512]{1,3,2,0:T(8,128)(2,1)} %bitcast.773) | data formatting | bytes 8388608 | tf_op jit(solution)/shard_map/stack;reshape | solution.py:304
  435.7 8.7 %pad_maximum_fusion = bf16[2,1024,4,512]{3,2,1,0:T(4,128)(2,1)} fusion(bf16[1,1024,4,512]{3,2,1,0:T(4,128)(2,1)} %copy.23, bf16[1,1024,4,512]{3,2,1,0:T(4,128)(2,1)} %copy.22), kind=kLoop, calls=%fused_computation | loop fusion | flops 4194304 | bytes 16777216 | tf_op jit(solution)/shard_map/stack | solution.py:304
  (366 shorter events, 87.6 us)
Async XLA Ops:
  0.6 7.9 %copy-start.17 = (bf16[2,1024,4,512]{3,2,1,0:T(4,128)(2,1)S(1)}, bf16[2,1024,4,512]{3,2,1,0:T(4,128)(2,1)}, u32[]{:S(2)}) copy-start(bf16[2,1024,4,512]{3,2,1,0:T(4,128)(2,1)} %param.8) | copy-start | bytes 25165828
  8.4 13.5 %copy-start.66 = (bf16[64,512]{1,0:T(8,128)(2,1)}, bf16[64,512]{1,0:T(8,128)(2,1)S(1)}, u32[]{:S(2)}) copy-start(bf16[64,512]{1,0:T(8,128)(2,1)S(1)} %get-tuple-element.29) | copy-start | bytes 196612
  8.4 13.5 %copy-start.68 = (bf16[64,512]{1,0:T(8,128)(2,1)}, bf16[64,512]{1,0:T(8,128)(2,1)S(1)}, u32[]{:S(2)}) copy-start(bf16[64,512]{1,0:T(8,128)(2,1)S(1)} %get-tuple-element.52) | copy-start | bytes 196612
  8.4 8.0 %slice-start = ((s8[8388608]{0:T(1024)(128)(4,1)}), s8[4194304]{0:T(1024)(128)(4,1)S(1)}, s32[]{:S(2)}) async-start(s8[8388608]{0:T(1024)(128)(4,1)} %bitcast.763), calls=%async_computation | async-start | bytes 8388608
  8.5 13.4 %copy-start.76 = (bf16[64,512]{1,0:T(8,128)(2,1)}, bf16[64,512]{1,0:T(8,128)(2,1)S(1)}, u32[]{:S(2)}) copy-start(bf16[64,512]{1,0:T(8,128)(2,1)S(1)} %get-tuple-element.80) | copy-start | bytes 196612
  8.5 13.4 %copy-start.78 = (bf16[64,512]{1,0:T(8,128)(2,1)}, bf16[64,512]{1,0:T(8,128)(2,1)S(1)}, u32[]{:S(2)}) copy-start(bf16[64,512]{1,0:T(8,128)(2,1)S(1)} %get-tuple-element.81) | copy-start | bytes 196612
  64.2 40.6 %copy-start.19 = (f32[64,4,512]{2,0,1:T(8,128)S(1)}, f32[64,4,512]{2,0,1:T(8,128)}, u32[]{:S(2)}) copy-start(f32[64,4,512]{2,0,1:T(8,128)} %get-tuple-element.90) | copy-start | bytes 1572868
  112.3 37.9 %copy-start.21 = (f32[64,4,512]{2,0,1:T(8,128)S(1)}, f32[64,4,512]{2,0,1:T(8,128)}, u32[]{:S(2)}) copy-start(f32[64,4,512]{2,0,1:T(8,128)} %get-tuple-element.88) | copy-start | bytes 1572868
  112.3 37.9 %copy-start.26 = (f32[64,512]{1,0:T(8,128)S(1)}, f32[64,512]{1,0:T(8,128)}, u32[]{:S(2)}) copy-start(f32[64,512]{1,0:T(8,128)} %copy-done.25) | copy-start | bytes 393220
  153.2 46.5 %copy-start.20 = (f32[64,4,512]{2,0,1:T(8,128)}, f32[64,4,512]{2,0,1:T(8,128)S(1)}, u32[]{:S(2)}) copy-start(f32[64,4,512]{2,0,1:T(8,128)S(1)} %get-tuple-element.86) | copy-start | bytes 1572868
  157.0 41.3 %copy-start.28 = (f32[64,512]{1,0:T(8,128)S(1)}, f32[64,512]{1,0:T(8,128)}, u32[]{:S(2)}) copy-start(f32[64,512]{1,0:T(8,128)} %copy-done.27) | copy-start | bytes 393220
  205.0 38.0 %copy-start.24 = (f32[64,512]{1,0:T(8,128)S(1)}, f32[64,512]{1,0:T(8,128)}, u32[]{:S(2)}) copy-start(f32[64,512]{1,0:T(8,128)} %copy-done.23) | copy-start | bytes 393220
  250.4 29.3 %copy-start.22 = (f32[64,4,512]{2,0,1:T(8,128)S(1)}, f32[64,4,512]{2,0,1:T(8,128)}, u32[]{:S(2)}) copy-start(f32[64,4,512]{2,0,1:T(8,128)} %get-tuple-element.82) | copy-start | bytes 1572868
  251.1 30.0 %copy-start.60 = (bf16[64,512]{1,0:T(8,128)(2,1)S(1)}, bf16[64,512]{1,0:T(8,128)(2,1)}, u32[]{:S(2)}) copy-start(bf16[64,512]{1,0:T(8,128)(2,1)} %copy-done.59) | copy-start | bytes 196612
  251.1 31.0 %copy-start.53 = (bf16[64,512]{1,0:T(8,128)(2,1)S(1)}, bf16[64,512]{1,0:T(8,128)(2,1)}, u32[]{:S(2)}) copy-start(bf16[64,512]{1,0:T(8,128)(2,1)} %copy-done.52) | copy-start | bytes 196612
  251.1 32.0 %copy-start.46 = (bf16[64,512]{1,0:T(8,128)(2,1)S(1)}, bf16[64,512]{1,0:T(8,128)(2,1)}, u32[]{:S(2)}) copy-start(bf16[64,512]{1,0:T(8,128)(2,1)} %copy-done.45) | copy-start | bytes 196612
  251.1 32.9 %copy-start.43 = (bf16[64,512]{1,0:T(8,128)(2,1)S(1)}, bf16[64,512]{1,0:T(8,128)(2,1)}, u32[]{:S(2)}) copy-start(bf16[64,512]{1,0:T(8,128)(2,1)} %copy-done.42) | copy-start | bytes 196612
  251.2 33.0 %copy-start.36 = (bf16[64,512]{1,0:T(8,128)(2,1)S(1)}, bf16[64,512]{1,0:T(8,128)(2,1)}, u32[]{:S(2)}) copy-start(bf16[64,512]{1,0:T(8,128)(2,1)} %copy-done.35) | copy-start | bytes 196612
  251.2 33.0 %copy-start.71 = (bf16[64,512]{1,0:T(8,128)(2,1)S(1)}, bf16[64,512]{1,0:T(8,128)(2,1)}, u32[]{:S(2)}) copy-start(bf16[64,512]{1,0:T(8,128)(2,1)} %copy-done.70) | copy-start | bytes 196612
  251.2 33.0 %copy-start.74 = (bf16[64,512]{1,0:T(8,128)(2,1)S(1)}, bf16[64,512]{1,0:T(8,128)(2,1)}, u32[]{:S(2)}) copy-start(bf16[64,512]{1,0:T(8,128)(2,1)} %copy-done.73) | copy-start | bytes 196612
  251.2 33.0 %copy-start.81 = (bf16[64,512]{1,0:T(8,128)(2,1)S(1)}, bf16[64,512]{1,0:T(8,128)(2,1)}, u32[]{:S(2)}) copy-start(bf16[64,512]{1,0:T(8,128)(2,1)} %copy-done.80) | copy-start | bytes 196612
  402.3 8.8 %copy-start.142 = (bf16[384,2048]{1,0:T(8,128)(2,1)S(1)}, bf16[384,2048]{1,0:T(8,128)(2,1)}, u32[]{:S(2)}) copy-start(bf16[384,2048]{1,0:T(8,128)(2,1)} %copy-done.141) | copy-start | bytes 4718596
  415.5 8.0 %copy-start.140 = (bf16[384,2048]{1,0:T(8,128)(2,1)S(1)}, bf16[384,2048]{1,0:T(8,128)(2,1)}, u32[]{:S(2)}) copy-start(bf16[384,2048]{1,0:T(8,128)(2,1)} %copy-done.139) | copy-start | bytes 4718596
  435.7 8.7 %copy-start.126 = (f32[6,64,512]{2,1,0:T(8,128)S(1)}, f32[6,64,512]{2,1,0:T(8,128)}, u32[]{:S(2)}) copy-start(f32[6,64,512]{2,1,0:T(8,128)} %get-tuple-element.99) | copy-start | bytes 2359300
  (121 other events, 470.4 us)
where the time goes:
time: 453 us; the launch traced here: 445 us
  Pallas kernels  259 us (57%)
  matrix products  72.4 us (16%)
  local copies, waits for them, and re-layouts  71.9 us (16%)
  other arithmetic  37.6 us (8%)
  between operations  4.91 us (1%)
    pallas_call x7, Pallas kernels, exchange(): pl.pallas_call(functools.partial(exchange_kernel, blocks, rows, cols, sca...  259 us
    dot_general x32, matrix products, contract(): lax.dot_general(left, right, ((dims, dims), ((), ())), preferred_element_...  72.4 us
    another operation x4, local copies, waits for them, and re-layouts, weight_grad(): jnp.stack([(contract(inputs[layer], flats[layer], (0,)) * scale).astype(j...  31.5 us
    another operation x2, other arithmetic, weight_grad(): jnp.stack([(contract(inputs[layer], flats[layer], (0,)) * scale).astype(j...  17.5 us
    another operation x24, other arithmetic  17 us
    unnamed x295, local copies, waits for them, and re-layouts  13.4 us
    squeeze x6, local copies, waits for them, and re-layouts, local(): gate_pre[layer, step]  11 us

commit v1 on v0

v1 whole, which is shorter than its diff:
```python
import functools

import jax
import jax.numpy as jnp
from jax import lax
from jax.experimental import pallas as pl
from jax.experimental.pallas import tpu as pltpu
from jax.sharding import PartitionSpec as P

MESH = pl.DeviceIdType.MESH
F32 = jnp.float32
BF16 = jnp.bfloat16
VMEM_BYTES = 60 * 1024 * 1024


def contract(left, right, dims):
    return lax.dot_general(left, right, ((dims[0], dims[1]), ((), ())), preferred_element_type=F32)


def tile_of(size, limit):
    while size % limit:
        limit //= 2
    return limit


def recurrence_kernel(
    rows, ratio, layers, steps,
    w_rec, w_in, gate_pre, cells, top_grad, gram,
    flats, input_grad, squares,
    rec_w, in_w, fac, carry, sq_acc, part, recv_a, acc, recv_b, gat, sq_mine, sq_a, sq_sum, sq_b,
    w_sem, sa, ra, sb, rb, sc, rc, qsa, qra, qsb, qrb,
):
    top = layers - 1
    diagonals = steps + top
    batch, units = top_grad.shape[1:]
    piece = batch // rows
    kind_in = layers
    row = lax.axis_index("row")
    col = lax.axis_index("col")
    deep, half = col // ratio, col % ratio

    def loads(layer):
        return (
            pltpu.make_async_copy(w_rec.at[layer], rec_w.at[layer], w_sem.at[0, layer]),
            pltpu.make_async_copy(w_in.at[layer], in_w.at[layer], w_sem.at[1, layer]),
        )

    for layer in range(top, -1, -1):
        for copy in loads(layer):
            copy.start()

    plane = [(dr, dh) for dr in range(rows) for dh in range(ratio)][1:]
    slot_of = {offset: index for index, offset in enumerate(plane)}

    def plane_peer(dr, dh):
        return ((row + dr) % rows, deep * ratio + (half + dh) % ratio)

    def line_peer(dz):
        return (row, ((deep + dz) % rows) * ratio + half)

    def row_peer(dq):
        return ((row + dq) % rows, col)

    barrier = pltpu.get_barrier_semaphore()
    for offset in plane:
        pl.semaphore_signal(barrier, inc=1, device_id=plane_peer(*offset), device_id_type=MESH)
    for dz in range(1, rows):
        pl.semaphore_signal(barrier, inc=1, device_id=line_peer(dz), device_id_type=MESH)
    pl.semaphore_wait(barrier, len(plane) + rows - 1)

    def remote(src, dst, send, recv, device):
        return pltpu.make_async_remote_copy(
            src_ref=src, dst_ref=dst, send_sem=send, recv_sem=recv, device_id=device, device_id_type=MESH
        )

    def quarter(index):
        return pl.ds(pl.multiple_of(index * piece, piece), piece)

    def lanes(index, size):
        return pl.ds(pl.multiple_of(index * size, size), size)

    def copy_a(kind, d, offset):
        dr, dh = offset
        slot = slot_of[offset]
        src = part.at[kind, d, quarter((row + dr) % rows), lanes((half + dh) % ratio, units)]
        return remote(src, recv_a.at[kind, d, slot], sa.at[kind, d, slot], ra.at[kind, d, slot], plane_peer(dr, dh))

    def copy_b(kind, d, dz):
        src = acc.at[kind, d, (deep + dz) % rows]
        return remote(src, recv_b.at[kind, d, dz - 1], sb.at[kind, d, dz - 1], rb.at[kind, d, dz - 1], line_peer(dz))

    def copy_c(kind, d, dq):
        spot = gat.at[kind, d, quarter(row)]
        return remote(spot, spot, sc.at[kind, d, dq - 1], rc.at[kind, d, dq - 1], row_peer(dq))

    def start_a(kind, d):
        for offset in plane:
            copy_a(kind, d, offset).start()

    def finish_a(kind, d):
        for offset in plane:
            copy_a(kind, d, offset).wait_recv()
        for dr in range(rows):
            value = None
            for dh in range(ratio):
                if dr == 0 and dh == 0:
                    new = part[kind, d, quarter(row), lanes(half, units)]
                else:
                    new = recv_a[kind, d, slot_of[(dr, dh)]]
                value = new if value is None else value + new
            acc[kind, d, (row - dr + rows) % rows] = value
        for dz in range(1, rows):
            copy_b(kind, d, dz).start()

    def finish_b(kind, d):
        value = acc[kind, d, deep]
        for dz in range(1, rows):
            copy_b(kind, d, dz).wait_recv()
            value = value + recv_b[kind, d, dz - 1]
        gat[kind, d, quarter(row)] = value
        for dq in range(1, rows):
            copy_c(kind, d, dq).start()

    def finish_c(kind, d):
        for dq in range(1, rows):
            spot = gat.at[kind, d, quarter((row - dq + rows) % rows)]
            remote(spot, spot, sc.at[kind, d, dq - 1], rc.at[kind, d, dq - 1], row_peer(dq)).wait_recv()

    def sent(kind, d):
        for offset in plane:
            copy_a(kind, d, offset).wait_send()
        for dz in range(1, rows):
            copy_b(kind, d, dz).wait_send()
        for dq in range(1, rows):
            copy_c(kind, d, dq).wait_send()

    def step_of(layer, d):
        return steps - 1 - d + top - layer

    def active(layer, d):
        return (d >= top - layer) & (d <= top - layer + steps - 1)

    def feeds(layer, d):
        first = top - layer - 1 if layer < top else 0
        return (d >= first) & (d <= top - layer + steps - 2)

    chunk = 16

    def factors(layer, step):
        def body(index, _):
            at = pl.ds(pl.multiple_of(index * chunk, chunk), chunk)
            in_gate = jax.nn.sigmoid(gate_pre[layer, step, 0, at, :])
            forget = jax.nn.sigmoid(gate_pre[layer, step, 1, at, :])
            cand = jnp.tanh(gate_pre[layer, step, 2, at, :])
            out_gate = jax.nn.sigmoid(gate_pre[layer, step, 3, at, :])
            tanh_cell = jnp.tanh(cells[layer, step + 1, at, :])
            fac[layer, 0, at, :] = out_gate * (1.0 - tanh_cell * tanh_cell)
            fac[layer, 1, at, :] = cand * in_gate * (1.0 - in_gate)
            fac[layer, 2, at, :] = cells[layer, step, at, :] * forget * (1.0 - forget)
            fac[layer, 3, at, :] = in_gate * (1.0 - cand * cand)
            fac[layer, 4, at, :] = tanh_cell * out_gate * (1.0 - out_gate)
            fac[layer, 5, at, :] = forget
            return 0

        lax.fori_loop(0, batch // chunk, body, 0)

    def cell(layer, d, step):
        def body(index, _):
            at = pl.ds(pl.multiple_of(index * chunk, chunk), chunk)
            out_at = pl.ds(pl.multiple_of(step * batch + index * chunk, chunk), chunk)
            if layer == top:
                hid = top_grad[step, at, :] + gat[layer, d, at, :]
            else:
                hid = gat[layer, d, at, :]
            grad = carry[layer, at, :] + hid * fac[layer, 0, at, :]
            for gate in range(3):
                flats[layer, out_at, gate * units:(gate + 1) * units] = (grad * fac[layer, gate + 1, at, :]).astype(BF16)
            flats[layer, out_at, 3 * units:] = (hid * fac[layer, 4, at, :]).astype(BF16)
            carry[layer, at, :] = grad * fac[layer, 5, at, :]
            return 0

        lax.fori_loop(0, batch // chunk, body, 0)

    outs = part.shape[-1]
    wide = tile_of(outs, 256)

    def product(weights, layer, step, kind, d, add):
        at = pl.ds(pl.multiple_of(step * batch, batch), batch)

        def body(index, _):
            spot = pl.ds(pl.multiple_of(index * wide, wide), wide)
            value = part[kind, d, :, spot] if add else None
            for gate in range(4):
                new = contract(flats[layer, at, gate * units:(gate + 1) * units], weights[layer, gate, spot, :], ((1,), (1,)))
                value = new if value is None else value + new
            part[kind, d, :, spot] = value
            return 0

        lax.fori_loop(0, outs // wide, body, 0)

    def grams(layer, step):
        at = pl.ds(pl.multiple_of(step * batch, batch), batch)

        def body(other, _):
            there = pl.ds(pl.multiple_of(other * batch, batch), batch)
            both = contract(flats[layer, at, :], flats[layer, there, :], ((1,), (1,)))
            weight = jnp.where(other == step, 1.0, 2.0).astype(F32)
            sq_acc[...] = sq_acc[...] + weight * (both * gram[layer, step, other])
            return 0

        lax.fori_loop(step, steps, body, 0)

    carry[...] = jnp.zeros_like(carry)
    sq_acc[...] = jnp.zeros_like(sq_acc)
    gat[top, diagonals] = jnp.zeros(gat.shape[2:], F32)
    factors(top, steps - 1)

    def diagonal(d, _):
        for layer in range(top, -1, -1):
            step = step_of(layer, d)

            @pl.when(active(layer, d))
            def _(layer=layer, step=step):
                before = d - 1
                if layer == top:
                    before = jnp.where(d == 0, diagonals, d - 1)

                    @pl.when(d > 0)
                    def _():
                        finish_c(layer, d - 1)
                else:
                    finish_c(layer, d - 1)
                cell(layer, before, step)

                @pl.when(d == top - layer)
                def _():
                    for copy in loads(layer):
                        copy.wait()

            @pl.when(feeds(layer, d))
            def _(layer=layer, step=step):
                if layer == top:
                    product(rec_w, layer, step, layer, d, False)
                else:
                    product(in_w, layer + 1, step_of(layer + 1, d), layer, d, False)

                    @pl.when(step < steps)
                    def _():
                        product(rec_w, layer, step, layer, d, True)

                start_a(layer, d)

        for layer in range(top, -1, -1):
            @pl.when(feeds(layer, d))
            def _(layer=layer):
                finish_a(layer, d)

        @pl.when(d >= top + 1)
        def _():
            finish_b(kind_in, d - 1)

        @pl.when(d >= top)
        def _():
            product(in_w, 0, step_of(0, d), kind_in, d, False)
            start_a(kind_in, d)

        for layer in range(top, -1, -1):
            @pl.when(active(layer, d))
            def _(layer=layer):
                grams(layer, step_of(layer, d))

            @pl.when(active(layer, d + 1))
            def _(layer=layer):
                factors(layer, step_of(layer, d + 1))

        @pl.when(d == diagonals - 1)
        def _():
            sq_mine[...] = jnp.full(sq_mine.shape, jnp.sum(sq_acc[...]), F32)
            for offset in plane:
                sq_copy_a(offset).start()

        for layer in range(top, -1, -1):
            @pl.when(feeds(layer, d))
            def _(layer=layer):
                finish_b(layer, d)

        @pl.when(d >= top)
        def _():
            finish_a(kind_in, d)

        return 0

    def sq_copy_a(offset):
        slot = slot_of[offset]
        return remote(sq_mine, sq_a.at[slot], qsa.at[slot], qra.at[slot], plane_peer(*offset))

    def sq_copy_b(dz):
        return remote(sq_sum, sq_b.at[dz - 1], qsb.at[dz - 1], qrb.at[dz - 1], line_peer(dz))

    lax.fori_loop(0, diagonals, diagonal, 0)

    value = sq_mine[...]
    for offset in plane:
        sq_copy_a(offset).wait_recv()
        value = value + sq_a[slot_of[offset]]
    sq_sum[...] = value
    for dz in range(1, rows):
        sq_copy_b(dz).start()
    finish_b(kind_in, diagonals - 1)
    value = sq_sum[...]
    for dz in range(1, rows):
        sq_copy_b(dz).wait_recv()
        value = value + sq_b[dz - 1]
    squares[...] = value

    def collect(d, _):
        finish_c(kind_in, d)
        input_grad[step_of(0, d)] = gat[kind_in, d]
        sent(kind_in, d)
        return 0

    lax.fori_loop(top, diagonals, collect, 0)

    def settle(d, _):
        for layer in range(layers):
            @pl.when(feeds(layer, d))
            def _(layer=layer):
                sent(layer, d)

        return 0

    lax.fori_loop(0, diagonals, settle, 0)
    for offset in plane:
        sq_copy_a(offset).wait_send()
    for dz in range(1, rows):
        sq_copy_b(dz).wait_send()


def recurrence(w_rec, w_in, gate_pre, cells, top_grad, gram):
    rows, cols = lax.axis_size("row"), lax.axis_size("col")
    ratio = cols // rows
    layers, _, row_units, units = w_rec.shape
    steps, batch, _ = top_grad.shape
    diagonals = steps + layers - 1
    piece = batch // rows
    kinds = layers + 1
    group = rows * ratio - 1
    dma = pltpu.SemaphoreType.DMA
    vmem = lambda *shape: pltpu.VMEM(shape, F32)
    in_vmem = pl.BlockSpec(memory_space=pltpu.VMEM)
    in_any = pl.BlockSpec(memory_space=pl.ANY)
    return pl.pallas_call(
        functools.partial(recurrence_kernel, rows, ratio, layers, steps),
        out_shape=[
            jax.ShapeDtypeStruct((layers, steps * batch, 4 * units), BF16),
            jax.ShapeDtypeStruct((steps, batch, units), F32),
            jax.ShapeDtypeStruct((8, 128), F32),
        ],
        in_specs=[in_any, in_any, in_vmem, in_vmem, in_vmem, in_vmem],
        out_specs=[in_vmem] * 3,
        scratch_shapes=[
            pltpu.VMEM((layers, 4, row_units, units), BF16), pltpu.VMEM((layers, 4, row_units, units), BF16),
            vmem(layers, 6, batch, units), vmem(layers, batch, units), vmem(batch, batch),
            vmem(kinds, diagonals, batch, row_units), vmem(kinds, diagonals, group, piece, units),
            vmem(kinds, diagonals, rows, piece, units), vmem(kinds, diagonals, rows - 1, piece, units),
            vmem(kinds, diagonals + 1, batch, units),
            vmem(8, 128), vmem(group, 8, 128), vmem(8, 128), vmem(rows - 1, 8, 128),
            dma((2, layers)),
            dma((kinds, diagonals, group)), dma((kinds, diagonals, group)),
            dma((kinds, diagonals, rows - 1)), dma((kinds, diagonals, rows - 1)),
            dma((kinds, diagonals, rows - 1)), dma((kinds, diagonals, rows - 1)),
            dma((group,)), dma((group,)), dma((rows - 1,)), dma((rows - 1,)),
        ],
        compiler_params=pltpu.CompilerParams(collective_id=0, has_side_effects=True, vmem_limit_bytes=VMEM_BYTES),
        name="recurrence",
    )(w_rec, w_in, gate_pre, cells, top_grad, gram)


def weight_kernel(entries, squares, h_prev, layer_in, flats, rec_out, in_out, stage):
    scale = 1.0 / jnp.maximum(jnp.sqrt(squares[...] / entries), 0.05)
    tall, units = rec_out.shape[1], rec_out.shape[3]
    scale = jnp.broadcast_to(scale[:1, :1], (tall, units))
    for source, out in ((h_prev, rec_out), (layer_in, in_out)):
        left = source[0].T
        for gate in range(4):
            value = contract(left, flats[0, :, gate * units:(gate + 1) * units], ((1,), (0,))) * scale
            for lane in range(units // 128):
                stage[lane, pl.ds(gate, tall, stride=4), :] = value[:, lane * 128:(lane + 1) * 128]
        for lane in range(units // 128):
            out[0, :, :, lane * 128:(lane + 1) * 128] = stage[lane].astype(BF16).reshape(tall, 4, 128)


def weight_grads(squares, h_prev, layer_in, flats, entries):
    layers, tokens, row_units = h_prev.shape
    units = flats.shape[2] // 4
    tall = tile_of(row_units, 128)
    source = pl.BlockSpec((1, tokens, tall), lambda layer, tile: (layer, 0, tile))
    target = pl.BlockSpec((1, tall, 4, units), lambda layer, tile: (layer, tile, 0, 0))
    shape = jax.ShapeDtypeStruct((layers, row_units, 4, units), BF16)
    return pl.pallas_call(
        functools.partial(weight_kernel, entries),
        grid=(layers, row_units // tall),
        out_shape=[shape, shape],
        in_specs=[
            pl.BlockSpec((8, 128), lambda layer, tile: (0, 0)),
            source, source,
            pl.BlockSpec((1, tokens, 4 * units), lambda layer, tile: (layer, 0, 0)),
        ],
        out_specs=[target, target],
        scratch_shapes=[pltpu.VMEM((units // 128, 4 * tall, 128), F32)],
        name="weight_grads",
    )(squares, h_prev, layer_in, flats)


def local(w_rec, w_in, gate_pre, cells, layer_in, h_prev, top_grad):
    layers, row_units = w_rec.shape[:2]
    steps, batch, units = top_grad.shape
    rec_in = h_prev.reshape(layers, steps * batch, row_units)
    lay_in = layer_in.reshape(layers, steps * batch, row_units)
    gram = jnp.stack([
        contract(rec_in[layer], rec_in[layer], ((1,), (1,))) + contract(lay_in[layer], lay_in[layer], ((1,), (1,)))
        for layer in range(layers)
    ])
    gram = gram.reshape(layers, steps, batch, steps, batch).transpose(0, 1, 3, 2, 4)
    flats, input_grad, squares = recurrence(
        w_rec.transpose(0, 2, 1, 3), w_in.transpose(0, 2, 1, 3), gate_pre.transpose(0, 1, 3, 2, 4), cells, top_grad, gram
    )
    entries = 2.0 * layers * (row_units * lax.axis_size("row")) * (4 * units * lax.axis_size("col"))
    rec_grad, in_grad = weight_grads(squares, rec_in, lay_in, flats, entries)
    return (rec_grad, in_grad, input_grad)


def solution(mesh):
    placed = (
        P(None, "row", None, "col"),
        P(None, "row", None, "col"),
        P(None, None, None, None, "col"),
        P(None, None, None, "col"),
        P(None, None, None, "row"),
        P(None, None, None, "row"),
        P(None, None, "col"),
    )
    return jax.shard_map(
        local,
        mesh=mesh,
        in_specs=placed,
        out_specs=(P(None, "row", None, "col"), P(None, "row", None, "col"), P(None, None, "col")),
        check_vma=False,
    )
```

time: 453 us -> 192 us (0.42); the launches traced: 445 us -> 192 us
  Pallas kernels: 259 us -> 164 us
  matrix products: 72.4 us -> 2.38 us
  local copies, waits for them, and re-layouts: 71.9 us -> 23 us
  other arithmetic: 37.6 us -> 1.64 us
    pallas_call x7 -> x2, Pallas kernels: 259 us -> 164 us  [the longest x1 142 us: recurrence(): pl.pallas_call(functools.partial(recurrence_kernel, rows, ratio, layers,...]
    dot_general x32 -> x4, matrix products: 72.4 us -> 2.38 us  [contract(): lax.dot_general(left, right, ((dims[0], dims[1]), ((), ())), preferred_el...]
    another operation x26 -> x0, other arithmetic: 34.5 us -> none  [the longest x2 17.5 us: weight_grad(): jnp.stack([(contract(inputs[layer], flats[layer], (0,)) * scale).astype(j...]
    another operation x4, local copies, waits for them, and re-layouts: 31.5 us -> 1.08 us  [local(): jnp.stack([contract(rec_in[layer], rec_in[layer], ((1,), (1,))) + contrac...]
    slice x6 -> x2, local copies, waits for them, and re-layouts: 15.3 us -> 1.78 us  [the longest x1 1.64 us: local(): lay_in[layer]]
    transpose x0 -> x1, local copies, waits for them, and re-layouts: none -> 11.2 us  [local(): w_in.transpose(0, 2, 1, 3)]
    squeeze x6 -> x0, local copies, waits for them, and re-layouts: 11 us -> none  [local(): gate_pre[layer, step]]
    unnamed x295 -> x10, local copies, waits for them, and re-layouts: 13.4 us -> 8.93 us
where the time goes in v1:
time: 192 us
  Pallas kernels  164 us (85%)
  local copies, waits for them, and re-layouts  23 us (12%)
  matrix products  2.38 us (1%)
    pallas_call x1, Pallas kernels, recurrence(): pl.pallas_call(functools.partial(recurrence_kernel, rows, ratio, layers,...  142 us
    pallas_call x1, Pallas kernels, weight_grads(): pl.pallas_call(functools.partial(weight_kernel, entries), grid=(layers, r...  22 us
    transpose x1, local copies, waits for them, and re-layouts, local(): w_in.transpose(0, 2, 1, 3)  11.2 us
    unnamed x10, local copies, waits for them, and re-layouts  8.93 us

profile of v1, /device:TPU:0, one launch (start us, length us, event | category | flops | bytes accessed | tf_op | source)
XLA Modules:
  0.0 191.5 jit_solution(8886085310746847362)
XLA Ops:
  0.6 0.0 copy-start
  0.6 1.6 fusion
  2.3 0.2 copy-done
  2.5 0.1 fusion.1
  2.7 0.6 fusion.2
  3.3 0.6 convolution_add_fusion.1
  3.9 0.6 fusion.3
  4.5 0.6 convolution_add_fusion
  5.1 0.3 stack.10
  5.4 0.2 copy.17
  5.6 0.3 stack.9
  6.0 0.2 copy.16
  6.2 0.0 slice-start
  6.2 1.6 maximum_bitcast_fusion.gram
  7.8 0.0 slice-start.1
  7.8 7.8 %copy.21 = f32[2,6,64,4,512]{4,2,3,1,0:T(8,128)} copy(f32[2,6,64,4,512]{4,3,2,1,0:T(4,128)} %param.9) | data formatting | bytes 12582912 | tf_op args[2]
  15.6 0.0 slice-done
  15.6 0.0 slice-done.1
  15.6 11.2 %copy_bitcast_fusion = (bf16[2,4,1024,512]{3,2,1,0:T(8,128)(2,1)}, bf16[2,4,1024,512]{3,2,1,0:T(8,128)(2,1)}) fusion(bf16[2,1024,4,512]{3,2,1,0:T(4,128)(2,1)S(1)} %bitcast.25, bf16[2,1024,4,512]{3,2,1,0:T(4,128)(2,1)} %param.7), kind=kLoop, calls=%fused_computation | loop fusion | bytes 33554432 | tf_op jit(solution)/shard_map/transpose | solution.py:426
  26.9 141.7 %recurrence.1 = (bf16[2,384,2048]{2,1,0:T(8,128)(2,1)}, f32[6,64,512]{2,1,0:T(8,128)}, f32[8,128]{1,0:T(8,128)}) custom-call(bf16[2,4,1024,512]{3,2,1,0:T(8,128)(2,1)} %get-tuple-element.18.w_rec, bf16[2,4,1024,512]{3,2,1,0:T(8,128)(2,1)} %get-tuple-element.17.w_in, f32[2,6,4,64,512]{4,3,2,1,0:T(8,128)} %bitcast.23, f32[2,7,64,512]{3,2,1,0:T(8,128)} %cells.1, ...), custom_call_target="tpu_custom_call" | custom-call | tf_op jit(solution)/shard_map/recurrence/pallas_call | solution.py:352
  168.6 0.0 copy-start.1
  168.6 22.0 %weight_grads.1 = (bf16[2,1024,4,512]{3,2,1,0:T(4,128)(2,1)}, bf16[2,1024,4,512]{3,2,1,0:T(4,128)(2,1)}) custom-call(f32[8,128]{1,0:T(8,128)} %get-tuple-element.8.squares, bf16[2,384,1024]{2,1,0:T(8,128)(2,1)} %bitcast.30, bf16[2,384,1024]{2,1,0:T(8,128)(2,1)} %bitcast.31, bf16[2,384,2048]{2,1,0:T(8,128)(2,1)} %get-tuple-element.9.flats), custom_call_target="tpu_custom_call" | custom-call | tf_op jit(solution)/shard_map/weight_grads/pallas_call | solution.py:400
  190.6 0.0 copy-done.1
  190.6 0.9 copy.23
  (1 shorter events, 0.0 us)
Async XLA Ops:
  0.6 1.9 copy-start
  6.2 9.5 %slice-start = ((s8[8388608]{0:T(1024)(128)(4,1)}), s8[4194304]{0:T(1024)(128)(4,1)S(1)}, s32[]{:S(2)}) async-start(s8[8388608]{0:T(1024)(128)(4,1)} %bitcast.24), calls=%async_computation | async-start | bytes 8388608
  7.8 7.8 %slice-start.1 = ((s8[8388608]{0:T(1024)(128)(4,1)}), s8[4194304]{0:T(1024)(128)(4,1)S(1)}, s32[]{:S(2)}) async-start(s8[8388608]{0:T(1024)(128)(4,1)} %bitcast.24), calls=%async_computation.1 | async-start | bytes 8388608
  168.6 22.0 %copy-start.1 = (f32[6,64,512]{2,1,0:T(8,128)S(1)}, f32[6,64,512]{2,1,0:T(8,128)}, u32[]{:S(2)}) copy-start(f32[6,64,512]{2,1,0:T(8,128)} %get-tuple-element.24) | copy-start | bytes 2359300

commit v2 on v1

v2 whole, which is shorter than its diff:
```python
import functools

import jax
import jax.numpy as jnp
from jax import lax
from jax.experimental import pallas as pl
from jax.experimental.pallas import tpu as pltpu
from jax.sharding import PartitionSpec as P

MESH = pl.DeviceIdType.MESH
F32 = jnp.float32
BF16 = jnp.bfloat16
VMEM_BYTES = 60 * 1024 * 1024


def contract(left, right, dims):
    return lax.dot_general(left, right, ((dims[0], dims[1]), ((), ())), preferred_element_type=F32)


def tile_of(size, limit):
    while size % limit:
        limit //= 2
    return limit


def recurrence_kernel(
    rows, cores, ratio, layers, steps,
    w_rec, w_in, gate_pre_any, cells_any, top_grad_any, h_prev_any, layer_in_any,
    flats, input_grad, squares,
    rec_w, in_w, raw, fold, gate_pre, cells, top_grad, h_prev, layer_in, fac, carry, sq_acc, part, recv_a, acc, recv_r, recv_b, gat, sq_mine, sq_a, sq_sum, sq_b,
    w_sem, e_sem, sa, ra, sr, rr, sb, rb, sc, rc, qsa, qra, qsb, qrb,
):
    top = layers - 1
    diagonals = steps + top
    batch, units = top_grad_any.shape[1:]
    piece = batch // rows
    kind_in = layers
    row = lax.axis_index("row")
    col = lax.axis_index("col")
    deep, half = col // ratio, col % ratio
    lots = rows // cores
    lot, core = row // cores, row % cores
    inside = core == deep % cores

    def load(which, layer):
        return pltpu.make_async_copy((w_rec, w_in)[which].at[layer], raw.at[which], w_sem.at[which])

    def move(src, dst, at, index):
        return pltpu.make_async_copy(src.at[at], dst.at[at], e_sem.at[index])

    late = steps - 1
    early = [
        move(gate_pre_any, gate_pre, (top, late), 0),
        move(cells_any, cells, top, 1),
        move(top_grad_any, top_grad, slice(None), 2),
    ]
    rest = [move(gate_pre_any, gate_pre, (top, slice(0, late)), 3)] if late else []
    for layer in range(top):
        rest.append(move(gate_pre_any, gate_pre, layer, 4 + 2 * layer))
        rest.append(move(cells_any, cells, layer, 5 + 2 * layer))
    rest.append(move(h_prev_any, h_prev, slice(None), 4 + 2 * top))
    rest.append(move(layer_in_any, layer_in, slice(None), 5 + 2 * top))
    for copy in early:
        copy.start()
    for which in range(2):
        load(which, top).start()
    for copy in rest:
        copy.start()

    plane = [(dr, dh) for dr in range(rows) for dh in range(ratio)][1:]
    slot_of = {offset: index for index, offset in enumerate(plane)}

    def plane_peer(dr, dh):
        return ((row + dr) % rows, deep * ratio + (half + dh) % ratio)

    def line_peer(dz):
        return (row, ((deep + dz) % rows) * ratio + half)

    def row_peer(dq):
        return ((row + dq) % rows, col)

    barrier = pltpu.get_barrier_semaphore()
    for offset in plane:
        pl.semaphore_signal(barrier, inc=1, device_id=plane_peer(*offset), device_id_type=MESH)
    for dz in range(1, rows):
        pl.semaphore_signal(barrier, inc=1, device_id=line_peer(dz), device_id_type=MESH)
    for dz in range(rows):
        source = (lot * cores + deep % cores, ((deep - dz + rows) % rows) * ratio + half)
        if dz:
            pl.semaphore_signal(barrier, inc=1, device_id=source, device_id_type=MESH)
        else:
            @pl.when(jnp.logical_not(inside))
            def _(source=source):
                pl.semaphore_signal(barrier, inc=1, device_id=source, device_id_type=MESH)

    pl.semaphore_wait(barrier, len(plane) + rows - 1 + rows - jnp.where(inside, 1, 0))

    def remote(src, dst, send, recv, device):
        return pltpu.make_async_remote_copy(
            src_ref=src, dst_ref=dst, send_sem=send, recv_sem=recv, device_id=device, device_id_type=MESH
        )

    def quarter(index):
        return pl.ds(pl.multiple_of(index * piece, piece), piece)

    def lanes(index, size):
        return pl.ds(pl.multiple_of(index * size, size), size)

    turns = [(dx, dg) for dx in list(range(1, lots)) + [0] for dg in list(range(1, cores)) + [0]]

    def block_of(dx, dg):
        return ((lot + dx) % lots) * cores + (core + dg) % cores

    def copy_a(kind, d, dh, dx, dg):
        src = part.at[kind, d, quarter(block_of(dx, dg)), lanes((half + dh) % ratio, units)]
        spot = (kind, d, dh - 1, dx, dg)
        return remote(src, recv_a.at[spot], sa.at[spot], ra.at[spot], plane_peer(0, dh))

    def copy_r(kind, d, dx, dg):
        spot = (kind, d, dx - 1, dg)
        return remote(acc.at[kind, d, dx, dg], recv_r.at[spot], sr.at[spot], rr.at[spot], (block_of(dx, 0), col))

    def origin(dx):
        return block_of(lots - dx, 0)

    def copy_b(kind, d, dx, dg):
        src = recv_r.at[kind, d, dx - 1, dg] if dx else acc.at[kind, d, 0, dg]
        slot = (origin(dx) - deep + rows) % rows
        peer = (block_of(0, dg), origin(dx) * ratio + half)
        return remote(src, recv_b.at[kind, d, slot], sb.at[kind, d, dx, dg], rb.at[kind, d, slot], peer)

    def copy_c(kind, d, dq):
        spot = gat.at[kind, d, quarter(row)]
        return remote(spot, spot, sc.at[kind, d, dq - 1], rc.at[kind, d, dq - 1], row_peer(dq))

    def start_a(kind, d, dh):
        for dx, dg in turns:
            copy_a(kind, d, dh, dx, dg).start()

    def finish_a(kind, d):
        for dx, dg in turns:
            value = part[kind, d, quarter(block_of(dx, dg)), lanes(half, units)]
            for dh in range(1, ratio):
                copy_a(kind, d, dh, dx, dg).wait_recv()
                value = value + recv_a[kind, d, dh - 1, dx, dg]
            if dx:
                acc[kind, d, dx, dg] = value
                copy_r(kind, d, dx, dg).start()
            elif dg:
                acc[kind, d, 0, dg] = value
                copy_b(kind, d, 0, dg).start()
            else:
                home = row == deep

                @pl.when(home)
                def _():
                    recv_b[kind, d, 0] = value

                @pl.when(jnp.logical_not(home))
                def _():
                    acc[kind, d, 0, 0] = value
                    copy_b(kind, d, 0, 0).start()

    def finish_r(kind, d):
        for dx in range(1, lots):
            for dg in list(range(1, cores)) + [0]:
                copy_r(kind, d, dx, dg).wait_recv()
                if dg:
                    copy_b(kind, d, dx, dg).start()
                else:
                    home = origin(dx) == deep

                    @pl.when(home)
                    def _():
                        recv_b[kind, d, 0] = recv_r[kind, d, dx - 1, 0]

                    @pl.when(jnp.logical_not(home))
                    def _():
                        copy_b(kind, d, dx, 0).start()

    def source_of(dz):
        return (lot * cores + deep % cores, ((deep - dz + rows) % rows) * ratio + half)

    def arrival(kind, d, dz):
        return remote(acc.at[kind, d, 0, 0], recv_b.at[kind, d, dz], sb.at[kind, d, 0, 0], rb.at[kind, d, dz], source_of(dz))

    def finish_b(kind, d):
        @pl.when(jnp.logical_not(inside))
        def _():
            arrival(kind, d, 0).wait_recv()

        for dz in range(1, rows):
            arrival(kind, d, dz).wait_recv()
        value = recv_b[kind, d, 0]
        for dz in range(1, rows):
            value = value + recv_b[kind, d, dz]
        gat[kind, d, quarter(row)] = value
        for dq in range(1, rows):
            copy_c(kind, d, dq).start()

    def finish_c(kind, d):
        for dq in range(1, rows):
            spot = gat.at[kind, d, quarter((row - dq + rows) % rows)]
            remote(spot, spot, sc.at[kind, d, dq - 1], rc.at[kind, d, dq - 1], row_peer(dq)).wait_recv()

    def sent(kind, d):
        for dx, dg in turns:
            for dh in range(1, ratio):
                copy_a(kind, d, dh, dx, dg).wait_send()
            if dx:
                copy_r(kind, d, dx, dg).wait_send()
            if dg:
                copy_b(kind, d, dx, dg).wait_send()
            else:
                @pl.when(origin(dx) != deep)
                def _(dx=dx):
                    copy_b(kind, d, dx, 0).wait_send()

        for dq in range(1, rows):
            copy_c(kind, d, dq).wait_send()

    def step_of(layer, d):
        return steps - 1 - d + top - layer

    def active(layer, d):
        return both(d >= top - layer, d <= top - layer + steps - 1)

    def feeds(layer, d):
        first = top - layer - 1 if layer < top else 0
        return both(d >= first, d <= top - layer + steps - 2)

    chunk = 16

    def factors(layer, step):
        def body(index, _):
            at = pl.ds(pl.multiple_of(index * chunk, chunk), chunk)
            in_gate = jax.nn.sigmoid(gate_pre[layer, step, at, 0, :])
            forget = jax.nn.sigmoid(gate_pre[layer, step, at, 1, :])
            cand = jnp.tanh(gate_pre[layer, step, at, 2, :])
            out_gate = jax.nn.sigmoid(gate_pre[layer, step, at, 3, :])
            tanh_cell = jnp.tanh(cells[layer, step + 1, at, :])
            fac[layer, 0, at, :] = out_gate * (1.0 - tanh_cell * tanh_cell)
            fac[layer, 1, at, :] = cand * in_gate * (1.0 - in_gate)
            fac[layer, 2, at, :] = cells[layer, step, at, :] * forget * (1.0 - forget)
            fac[layer, 3, at, :] = in_gate * (1.0 - cand * cand)
            fac[layer, 4, at, :] = tanh_cell * out_gate * (1.0 - out_gate)
            fac[layer, 5, at, :] = forget
            return 0

        lax.fori_loop(0, batch // chunk, body, 0)

    def cell(layer, d, step):
        def body(index, _):
            at = pl.ds(pl.multiple_of(index * chunk, chunk), chunk)
            out_at = pl.ds(pl.multiple_of(step * batch + index * chunk, chunk), chunk)
            if layer == top:
                hid = top_grad[step, at, :] + gat[layer, d, at, :]
            else:
                hid = gat[layer, d, at, :]
            grad = carry[layer, at, :] + hid * fac[layer, 0, at, :]
            for gate in range(3):
                flats[layer, out_at, gate * units:(gate + 1) * units] = (grad * fac[layer, gate + 1, at, :]).astype(BF16)
            flats[layer, out_at, 3 * units:] = (hid * fac[layer, 4, at, :]).astype(BF16)
            carry[layer, at, :] = grad * fac[layer, 5, at, :]
            return 0

        lax.fori_loop(0, batch // chunk, body, 0)

    row_units = part.shape[-1]

    def rows_of(step):
        return pl.ds(step * batch if isinstance(step, int) else pl.multiple_of(step * batch, batch), batch)

    def product(weights, layer, step, kind, d, dh, add):
        at = rows_of(step)
        spot = lanes((half + dh) % ratio, units)
        value = part[kind, d, :, spot] if add else None
        for gate in range(4):
            new = contract(flats[layer, at, gate * units:(gate + 1) * units], weights[layer, gate, :, spot], ((1,), (0,)))
            value = new if value is None else value + new
        part[kind, d, :, spot] = value

    def send_product(weights, layer, step, kind, d, add):
        for dh in list(range(1, ratio)) + [0]:
            product(weights, layer, step, kind, d, dh, add)
            if dh:
                start_a(kind, d, dh)

    tall = 128

    def unfold(which, weights, layer):
        def body(index, _):
            at = pl.ds(pl.multiple_of(index * tall, tall), tall)
            for lane in range(units // 128):
                span = slice(lane * 128, (lane + 1) * 128)
                fold[lane] = raw[which, at, :, span].astype(F32).reshape(4 * tall, 128)
            for lane in range(units // 128):
                span = slice(lane * 128, (lane + 1) * 128)
                for gate in range(4):
                    weights[layer, gate, span, at] = fold[lane, pl.ds(gate, tall, stride=4), :].astype(BF16).T
            return 0

        lax.fori_loop(0, row_units // tall, body, 0)

    tokens = steps * batch

    def grams(layer, step):
        at = rows_of(step)
        both = contract(flats[layer, at, :], flats[layer], ((1,), (1,)))
        outer = contract(h_prev[layer, at, :], h_prev[layer], ((1,), (1,)))
        outer = outer + contract(layer_in[layer, at, :], layer_in[layer], ((1,), (1,)))
        other = lax.broadcasted_iota(jnp.int32, (batch, tokens), 1)
        first = step * batch
        weight = jnp.where((other >= first) & (other < first + batch), 1.0, 2.0).astype(F32)
        sq_acc[...] = sq_acc[...] + weight * (both * outer)

    carry[...] = jnp.zeros_like(carry)
    sq_acc[...] = jnp.zeros_like(sq_acc)
    gat[top, diagonals] = jnp.zeros(gat.shape[2:], F32)
    flats[...] = jnp.zeros_like(flats)
    for copy in early:
        copy.wait()
    factors(top, steps - 1)

    def take(layer, d):
        before = d - 1
        if layer == top:
            before = d - 1 if isinstance(d, int) else jnp.where(d == 0, diagonals, d - 1)
            when(d > 0, functools.partial(finish_c, layer, d - 1))
        else:
            finish_c(layer, d - 1)
        cell(layer, before, step_of(layer, d))

    def spread(layer, d):
        step = step_of(layer, d)
        if layer == top:
            send_product(rec_w, layer, step, layer, d, False)
            return

        def alone():
            for dh in range(1, ratio):
                start_a(layer, d, dh)

        when(step < steps, functools.partial(send_product, rec_w, layer, step, layer, d, True))
        when(step >= steps, alone)

    def ready(which, weights, layer):
        load(which, layer).wait()
        unfold(which, weights, layer)
        if layer > 0:
            load(which, layer - 1).start()

    def when(condition, step):
        if isinstance(condition, bool):
            if condition:
                step()
        else:
            pl.when(condition)(step)

    def both(first, second):
        return first and second if isinstance(first, bool) else first & second

    def running(d):
        return both(d >= top, d <= diagonals - 1)

    def opening(d):
        for layer in range(top, -1, -1):
            when(active(layer, d), functools.partial(take, layer, d))
            if layer == top:
                when(d == 0, functools.partial(ready, 0, rec_w, layer))
            when(feeds(layer, d), functools.partial(spread, layer, d))
            if layer == top:
                when(running(d - 1), functools.partial(finish_r, kind_in, d - 1))
            if layer > 0:
                def pass_down(layer=layer):
                    when(d == top - layer, functools.partial(ready, 1, in_w, layer))
                    for dh in range(ratio):
                        product(in_w, layer, step_of(layer, d), layer - 1, d, dh, False)

                when(feeds(layer - 1, d), pass_down)

        def bottom():
            when(d == top, functools.partial(ready, 1, in_w, 0))
            send_product(in_w, 0, step_of(0, d), kind_in, d, False)

        when(running(d), bottom)

    def fill_gram(layer, d):
        when(active(layer, d), functools.partial(grams, layer, step_of(layer, d)))

    def fill_factors(layer, d):
        when(active(layer, d + 1), functools.partial(factors, layer, step_of(layer, d + 1)))

    def diagonal(d, _):
        opening(d)
        for layer in range(top, -1, -1):
            when(feeds(layer, d), functools.partial(finish_a, layer, d))
            if layer == top:
                @pl.when(d == 0)
                def _():
                    for copy in rest:
                        copy.wait()

                fill_gram(layer, d)
            else:
                when(running(d - 1), functools.partial(finish_b, kind_in, d - 1))
                fill_factors(layer + 1, d)
            when(feeds(layer, d), functools.partial(finish_r, layer, d))
            if layer < top:
                when(d == top - layer - 1, functools.partial(ready, 0, rec_w, layer))
                fill_gram(layer, d)
        for layer in range(top, -1, -1):
            when(feeds(layer, d), functools.partial(finish_b, layer, d))
            if layer == top:
                when(running(d), functools.partial(finish_a, kind_in, d))
            if layer > 0:
                fill_factors(layer - 1, d)
        return 0

    def sq_copy_a(offset):
        slot = slot_of[offset]
        return remote(sq_mine, sq_a.at[slot], qsa.at[slot], qra.at[slot], plane_peer(*offset))

    def sq_copy_b(dz):
        return remote(sq_sum, sq_b.at[dz - 1], qsb.at[dz - 1], qrb.at[dz - 1], line_peer(dz))

    def collect(d):
        finish_c(kind_in, d)
        input_grad[step_of(0, d)] = gat[kind_in, d]

    def settle(d, _):
        for layer in range(layers):
            pl.when(feeds(layer, d))(functools.partial(sent, layer, d))
        return 0

    def settle_in(d, _):
        sent(kind_in, d)
        return 0

    final = diagonals - 1
    lax.fori_loop(0, final, diagonal, 0)
    opening(final)
    fill_gram(0, final)
    sq_mine[...] = jnp.full(sq_mine.shape, jnp.sum(sq_acc[...]), F32)
    for offset in plane:
        sq_copy_a(offset).start()
    finish_a(kind_in, final)
    value = sq_mine[...]
    for offset in plane:
        sq_copy_a(offset).wait_recv()
        value = value + sq_a[slot_of[offset]]
    sq_sum[...] = value
    for dz in range(1, rows):
        sq_copy_b(dz).start()
    finish_b(kind_in, final - 1)
    finish_r(kind_in, final)
    lax.fori_loop(0, diagonals, settle, 0)

    def gather(d, _):
        collect(d)
        return 0

    lax.fori_loop(top, final, gather, 0)
    value = sq_sum[...]
    for dz in range(1, rows):
        sq_copy_b(dz).wait_recv()
        value = value + sq_b[dz - 1]
    squares[...] = value
    for offset in plane:
        sq_copy_a(offset).wait_send()
    for dz in range(1, rows):
        sq_copy_b(dz).wait_send()
    finish_b(kind_in, final)
    lax.fori_loop(top, final, settle_in, 0)
    collect(final)
    sent(kind_in, final)


def recurrence(w_rec, w_in, gate_pre, cells, top_grad, h_prev, layer_in):
    rows, cols = lax.axis_size("row"), lax.axis_size("col")
    ratio = cols // rows
    layers, row_units, _, units = w_rec.shape
    steps, batch, _ = top_grad.shape
    diagonals = steps + layers - 1
    piece = batch // rows
    cores = 2 if rows % 2 == 0 else 1
    lots = rows // cores
    kinds = layers + 1
    group = rows * ratio - 1
    dma = pltpu.SemaphoreType.DMA
    vmem = lambda *shape: pltpu.VMEM(shape, F32)
    in_vmem = pl.BlockSpec(memory_space=pltpu.VMEM)
    in_any = pl.BlockSpec(memory_space=pl.ANY)
    return pl.pallas_call(
        functools.partial(recurrence_kernel, rows, cores, ratio, layers, steps),
        out_shape=[
            jax.ShapeDtypeStruct((layers, steps * batch, 4 * units), BF16),
            jax.ShapeDtypeStruct((steps, batch, units), F32),
            jax.ShapeDtypeStruct((8, 128), F32),
        ],
        in_specs=[in_any] * 7,
        out_specs=[in_vmem] * 3,
        scratch_shapes=[
            pltpu.VMEM((layers, 4, units, row_units), BF16), pltpu.VMEM((layers, 4, units, row_units), BF16),
            pltpu.VMEM((2, row_units, 4, units), BF16), vmem(units // 128, 4 * 128, 128),
            vmem(*gate_pre.shape), vmem(*cells.shape), vmem(*top_grad.shape),
            pltpu.VMEM(h_prev.shape, BF16), pltpu.VMEM(layer_in.shape, BF16),
            vmem(layers, 6, batch, units), vmem(layers, batch, units), vmem(batch, steps * batch),
            vmem(kinds, diagonals, batch, row_units), vmem(kinds, diagonals, ratio - 1, lots, cores, piece, units),
            vmem(kinds, diagonals, lots, cores, piece, units), vmem(kinds, diagonals, max(lots - 1, 1), cores, piece, units),
            vmem(kinds, diagonals, rows, piece, units),
            vmem(kinds, diagonals + 1, batch, units),
            vmem(8, 128), vmem(group, 8, 128), vmem(8, 128), vmem(rows - 1, 8, 128),
            dma((2,)), dma((4 + 2 * layers,)),
            dma((kinds, diagonals, ratio - 1, lots, cores)), dma((kinds, diagonals, ratio - 1, lots, cores)),
            dma((kinds, diagonals, max(lots - 1, 1), cores)), dma((kinds, diagonals, max(lots - 1, 1), cores)),
            dma((kinds, diagonals, lots, cores)), dma((kinds, diagonals, rows)),
            dma((kinds, diagonals, rows - 1)), dma((kinds, diagonals, rows - 1)),
            dma((group,)), dma((group,)), dma((rows - 1,)), dma((rows - 1,)),
        ],
        compiler_params=pltpu.CompilerParams(collective_id=0, has_side_effects=True, vmem_limit_bytes=VMEM_BYTES),
        name="recurrence",
    )(w_rec, w_in, gate_pre, cells, top_grad, h_prev, layer_in)


def weight_kernel(entries, squares, h_prev, layer_in, flats, rec_out, in_out, stage):
    scale = 1.0 / jnp.maximum(jnp.sqrt(squares[...] / entries), 0.05)
    tall, units = rec_out.shape[1], rec_out.shape[3]
    scale = jnp.broadcast_to(scale[:1, :1], (tall, units))
    for source, out in ((h_prev, rec_out), (layer_in, in_out)):
        left = source[0].T
        for gate in range(4):
            value = contract(left, flats[0, :, gate * units:(gate + 1) * units], ((1,), (0,))) * scale
            for lane in range(units // 128):
                stage[lane, pl.ds(gate, tall, stride=4), :] = value[:, lane * 128:(lane + 1) * 128]
        for lane in range(units // 128):
            out[0, :, :, lane * 128:(lane + 1) * 128] = stage[lane].reshape(tall, 4, 128).astype(BF16)


def weight_grads(squares, h_prev, layer_in, flats, entries):
    layers, tokens, row_units = h_prev.shape
    units = flats.shape[2] // 4
    tall = tile_of(row_units, 512)
    source = pl.BlockSpec((1, tokens, tall), lambda layer, tile: (layer, 0, tile))
    target = pl.BlockSpec((1, tall, 4, units), lambda layer, tile: (layer, tile, 0, 0))
    shape = jax.ShapeDtypeStruct((layers, row_units, 4, units), BF16)
    return pl.pallas_call(
        functools.partial(weight_kernel, entries),
        grid=(layers, row_units // tall),
        out_shape=[shape, shape],
        in_specs=[
            pl.BlockSpec((8, 128), lambda layer, tile: (0, 0)),
            source, source,
            pl.BlockSpec((1, tokens, 4 * units), lambda layer, tile: (layer, 0, 0)),
        ],
        out_specs=[target, target],
        scratch_shapes=[pltpu.VMEM((units // 128, 4 * tall, 128), F32)],
        compiler_params=pltpu.CompilerParams(vmem_limit_bytes=VMEM_BYTES),
        name="weight_grads",
    )(squares, h_prev, layer_in, flats)


def local(w_rec, w_in, gate_pre, cells, layer_in, h_prev, top_grad):
    layers, row_units = w_rec.shape[:2]
    steps, batch, units = top_grad.shape
    rec_in = h_prev.reshape(layers, steps * batch, row_units)
    lay_in = layer_in.reshape(layers, steps * batch, row_units)
    flats, input_grad, squares = recurrence(w_rec, w_in, gate_pre, cells, top_grad, rec_in, lay_in)
    entries = 2.0 * layers * (row_units * lax.axis_size("row")) * (4 * units * lax.axis_size("col"))
    rec_grad, in_grad = weight_grads(squares, rec_in, lay_in, flats, entries)
    return (rec_grad, in_grad, input_grad)


def solution(mesh):
    placed = (
        P(None, "row", None, "col"),
        P(None, "row", None, "col"),
        P(None, None, None, None, "col"),
        P(None, None, None, "col"),
        P(None, None, None, "row"),
        P(None, None, None, "row"),
        P(None, None, "col"),
    )
    return jax.shard_map(
        local,
        mesh=mesh,
        in_specs=placed,
        out_specs=(P(None, "row", None, "col"), P(None, "row", None, "col"), P(None, None, "col")),
        check_vma=False,
    )
```

time: 192 us -> 150 us (0.78)
  local copies, waits for them, and re-layouts: 23 us -> 0.88 us
  Pallas kernels: 164 us -> 148 us
  matrix products: 2.38 us -> 0 us
    pallas_call x1, Pallas kernels: 142 us -> 130 us  [recurrence(): pl.pallas_call(functools.partial(recurrence_kernel, rows, cores, ratio, l...]
    transpose x1 -> x0, local copies, waits for them, and re-layouts: 11.2 us -> none  [local(): w_in.transpose(0, 2, 1, 3)]
    unnamed x10 -> x3, local copies, waits for them, and re-layouts: 8.93 us -> 0.88 us
    pallas_call x1, Pallas kernels: 22 us -> 17.9 us  [weight_grads(): pl.pallas_call(functools.partial(weight_kernel, entries), grid=(layers, r...]
    dot_general x4 -> x0, matrix products: 2.38 us -> none  [contract(): lax.dot_general(left, right, ((dims[0], dims[1]), ((), ())), preferred_el...]
where the time goes in v2:
time: 150 us
  Pallas kernels  148 us (99%)
    pallas_call x1, Pallas kernels, recurrence(): pl.pallas_call(functools.partial(recurrence_kernel, rows, cores, ratio, l...  130 us
    pallas_call x1, Pallas kernels, weight_grads(): pl.pallas_call(functools.partial(weight_kernel, entries), grid=(layers, r...  17.9 us

profile of v2, /device:TPU:0, one launch (start us, length us, event | category | flops | bytes accessed | tf_op | source)
XLA Modules:
  0.0 149.6 jit_solution(9735293260149781722)
XLA Ops:
  0.6 130.2 %recurrence.1 = (bf16[2,384,2048]{2,1,0:T(8,128)(2,1)}, f32[6,64,512]{2,1,0:T(8,128)}, f32[8,128]{1,0:T(8,128)}) custom-call(bf16[2,1024,4,512]{3,2,1,0:T(4,128)(2,1)} %w_rec.1, bf16[2,1024,4,512]{3,2,1,0:T(4,128)(2,1)} %w_in.1, f32[2,6,64,4,512]{4,3,2,1,0:T(4,128)} %gate_pre_any.1, f32[2,7,64,512]{3,2,1,0:T(8,128)} %cells_any.1, ...), custom_call_target="tpu_custom_call" | custom-call | tf_op jit(solution)/shard_map/recurrence/pallas_call | solution.py:494
  130.8 0.0 copy-start
  130.8 17.9 %weight_grads.1 = (bf16[2,1024,4,512]{3,2,1,0:T(4,128)(2,1)}, bf16[2,1024,4,512]{3,2,1,0:T(4,128)(2,1)}) custom-call(f32[8,128]{1,0:T(8,128)} %get-tuple-element.8.squares, bf16[2,384,1024]{2,1,0:T(8,128)(2,1)} %bitcast.3, bf16[2,384,1024]{2,1,0:T(8,128)(2,1)} %bitcast.5, bf16[2,384,2048]{2,1,0:T(8,128)(2,1)} %get-tuple-element.9.flats), custom_call_target="tpu_custom_call" | custom-call | tf_op jit(solution)/shard_map/weight_grads/pallas_call | solution.py:547
  148.7 0.0 copy-done
  148.7 0.9 copy.11
Async XLA Ops:
  130.8 17.9 %copy-start = (f32[6,64,512]{2,1,0:T(8,128)S(1)}, f32[6,64,512]{2,1,0:T(8,128)}, u32[]{:S(2)}) copy-start(f32[6,64,512]{2,1,0:T(8,128)} %get-tuple-element.18) | copy-start | bytes 2359300

commit v3 on v2

--- a/solution.py
+++ b/solution.py
@@ -10,7 +10,7 @@
 MESH = pl.DeviceIdType.MESH
 F32 = jnp.float32
 BF16 = jnp.bfloat16
-VMEM_BYTES = 60 * 1024 * 1024
+VMEM_BYTES = 63 * 1024 * 1024
 
 
 def contract(left, right, dims):
@@ -93,7 +93,6 @@
             def _(source=source):
                 pl.semaphore_signal(barrier, inc=1, device_id=source, device_id_type=MESH)
 
-    pl.semaphore_wait(barrier, len(plane) + rows - 1 + rows - jnp.where(inside, 1, 0))
 
     def remote(src, dst, send, recv, device):
         return pltpu.make_async_remote_copy(
@@ -302,22 +301,15 @@
 
         lax.fori_loop(0, row_units // tall, body, 0)
 
-    tokens = steps * batch
-
-    def grams(layer, step):
-        at = rows_of(step)
-        both = contract(flats[layer, at, :], flats[layer], ((1,), (1,)))
-        outer = contract(h_prev[layer, at, :], h_prev[layer], ((1,), (1,)))
-        outer = outer + contract(layer_in[layer, at, :], layer_in[layer], ((1,), (1,)))
-        other = lax.broadcasted_iota(jnp.int32, (batch, tokens), 1)
-        first = step * batch
-        weight = jnp.where((other >= first) & (other < first + batch), 1.0, 2.0).astype(F32)
-        sq_acc[...] = sq_acc[...] + weight * (both * outer)
+
+    def grams(layer):
+        outer = contract(h_prev[layer], h_prev[layer], ((1,), (1,))) + contract(layer_in[layer], layer_in[layer], ((1,), (1,)))
+        whole = contract(flats[layer], flats[layer], ((1,), (1,)))
+        sq_acc[...] = sq_acc[...] + outer * whole
 
     carry[...] = jnp.zeros_like(carry)
     sq_acc[...] = jnp.zeros_like(sq_acc)
     gat[top, diagonals] = jnp.zeros(gat.shape[2:], F32)
-    flats[...] = jnp.zeros_like(flats)
     for copy in early:
         copy.wait()
     factors(top, steps - 1)
@@ -366,8 +358,6 @@
     def opening(d):
         for layer in range(top, -1, -1):
             when(active(layer, d), functools.partial(take, layer, d))
-            if layer == top:
-                when(d == 0, functools.partial(ready, 0, rec_w, layer))
             when(feeds(layer, d), functools.partial(spread, layer, d))
             if layer == top:
                 when(running(d - 1), functools.partial(finish_r, kind_in, d - 1))
@@ -383,19 +373,21 @@
             when(d == top, functools.partial(ready, 1, in_w, 0))
             send_product(in_w, 0, step_of(0, d), kind_in, d, False)
 
-        when(running(d), bottom)
+        return bottom
 
     def fill_gram(layer, d):
-        when(active(layer, d), functools.partial(grams, layer, step_of(layer, d)))
+        when(d == top - layer + steps - 1, functools.partial(grams, layer))
 
     def fill_factors(layer, d):
         when(active(layer, d + 1), functools.partial(factors, layer, step_of(layer, d + 1)))
 
     def diagonal(d, _):
-        opening(d)
+        bottom = opening(d)
         for layer in range(top, -1, -1):
             when(feeds(layer, d), functools.partial(finish_a, layer, d))
             if layer == top:
+                when(running(d), bottom)
+
                 @pl.when(d == 0)
                 def _():
                     for copy in rest:
@@ -438,8 +430,10 @@
         return 0
 
     final = diagonals - 1
+    ready(0, rec_w, top)
+    pl.semaphore_wait(barrier, len(plane) + rows - 1 + rows - jnp.where(inside, 1, 0))
     lax.fori_loop(0, final, diagonal, 0)
-    opening(final)
+    opening(final)()
     fill_gram(0, final)
     sq_mine[...] = jnp.full(sq_mine.shape, jnp.sum(sq_acc[...]), F32)
     for offset in plane:
@@ -505,7 +499,7 @@
             pltpu.VMEM((2, row_units, 4, units), BF16), vmem(units // 128, 4 * 128, 128),
             vmem(*gate_pre.shape), vmem(*cells.shape), vmem(*top_grad.shape),
             pltpu.VMEM(h_prev.shape, BF16), pltpu.VMEM(layer_in.shape, BF16),
-            vmem(layers, 6, batch, units), vmem(layers, batch, units), vmem(batch, steps * batch),
+            vmem(layers, 6, batch, units), vmem(layers, batch, units), vmem(steps * batch, steps * batch),
             vmem(kinds, diagonals, batch, row_units), vmem(kinds, diagonals, ratio - 1, lots, cores, piece, units),
             vmem(kinds, diagonals, lots, cores, piece, units), vmem(kinds, diagonals, max(lots - 1, 1), cores, piece, units),
             vmem(kinds, diagonals, rows, piece, units),
@@ -526,15 +520,19 @@
 def weight_kernel(entries, squares, h_prev, layer_in, flats, rec_out, in_out, stage):
     scale = 1.0 / jnp.maximum(jnp.sqrt(squares[...] / entries), 0.05)
     tall, units = rec_out.shape[1], rec_out.shape[3]
-    scale = jnp.broadcast_to(scale[:1, :1], (tall, units))
-    for source, out in ((h_prev, rec_out), (layer_in, in_out)):
-        left = source[0].T
+    wide = tile_of(units, 256)
+    scale = jnp.broadcast_to(scale[:1, :1], (2 * tall, wide))
+    left = jnp.concatenate([h_prev[0].T, layer_in[0].T], axis=0)
+    for tile in range(units // wide):
         for gate in range(4):
-            value = contract(left, flats[0, :, gate * units:(gate + 1) * units], ((1,), (0,))) * scale
-            for lane in range(units // 128):
-                stage[lane, pl.ds(gate, tall, stride=4), :] = value[:, lane * 128:(lane + 1) * 128]
-        for lane in range(units // 128):
-            out[0, :, :, lane * 128:(lane + 1) * 128] = stage[lane].reshape(tall, 4, 128).astype(BF16)
+            start = gate * units + tile * wide
+            value = contract(left, flats[0, :, start:start + wide], ((1,), (0,))) * scale
+            for lane in range(wide // 128):
+                stage[lane, pl.ds(gate, 2 * tall, stride=4), :] = value[:, lane * 128:(lane + 1) * 128]
+        for lane in range(wide // 128):
+            span = slice(tile * wide + lane * 128, tile * wide + (lane + 1) * 128)
+            rec_out[0, :, :, span] = stage[lane, :4 * tall].reshape(tall, 4, 128).astype(BF16)
+            in_out[0, :, :, span] = stage[lane, 4 * tall:].reshape(tall, 4, 128).astype(BF16)
 
 
 def weight_grads(squares, h_prev, layer_in, flats, entries):
@@ -554,7 +552,7 @@
             pl.BlockSpec((1, tokens, 4 * units), lambda layer, tile: (layer, 0, 0)),
         ],
         out_specs=[target, target],
-        scratch_shapes=[pltpu.VMEM((units // 128, 4 * tall, 128), F32)],
+        scratch_shapes=[pltpu.VMEM((tile_of(units, 256) // 128, 8 * tall, 128), F32)],
         compiler_params=pltpu.CompilerParams(vmem_limit_bytes=VMEM_BYTES),
         name="weight_grads",
     )(squares, h_prev, layer_in, flats)

time: 150 us -> 146 us (0.973)
  Pallas kernels: 148 us -> 144 us
    pallas_call x1, Pallas kernels: 130 us -> 127 us  [recurrence(): pl.pallas_call(functools.partial(recurrence_kernel, rows, cores, ratio, l...]
where the time goes in v3:
time: 146 us
  Pallas kernels  144 us (99%)
    pallas_call x1, Pallas kernels, recurrence(): pl.pallas_call(functools.partial(recurrence_kernel, rows, cores, ratio, l...  127 us
    pallas_call x1, Pallas kernels, weight_grads(): pl.pallas_call(functools.partial(weight_kernel, entries), grid=(layers, r...  16.6 us

profile of v3, /device:TPU:0, one launch (start us, length us, event | category | flops | bytes accessed | tf_op | source)
XLA Modules:
  0.0 145.6 jit_solution(17082623839850383862)
XLA Ops:
  0.6 127.4 %recurrence.1 = (bf16[2,384,2048]{2,1,0:T(8,128)(2,1)}, f32[6,64,512]{2,1,0:T(8,128)}, f32[8,128]{1,0:T(8,128)}) custom-call(bf16[2,1024,4,512]{3,2,1,0:T(4,128)(2,1)} %w_rec.1, bf16[2,1024,4,512]{3,2,1,0:T(4,128)(2,1)} %w_in.1, f32[2,6,64,4,512]{4,3,2,1,0:T(4,128)} %gate_pre_any.1, f32[2,7,64,512]{3,2,1,0:T(8,128)} %cells_any.1, ...), custom_call_target="tpu_custom_call" | custom-call | tf_op jit(solution)/shard_map/recurrence/pallas_call | solution.py:488
  128.0 0.0 copy-start
  128.0 16.6 %weight_grads.1 = (bf16[2,1024,4,512]{3,2,1,0:T(4,128)(2,1)}, bf16[2,1024,4,512]{3,2,1,0:T(4,128)(2,1)}) custom-call(f32[8,128]{1,0:T(8,128)} %get-tuple-element.8.squares, bf16[2,384,1024]{2,1,0:T(8,128)(2,1)} %bitcast.3, bf16[2,384,1024]{2,1,0:T(8,128)(2,1)} %bitcast.5, bf16[2,384,2048]{2,1,0:T(8,128)(2,1)} %get-tuple-element.9.flats), custom_call_target="tpu_custom_call" | custom-call | tf_op jit(solution)/shard_map/weight_grads/pallas_call | solution.py:545
  144.7 0.0 copy-done
  144.7 0.9 copy.11
Async XLA Ops:
  128.0 16.7 %copy-start = (f32[6,64,512]{2,1,0:T(8,128)S(1)}, f32[6,64,512]{2,1,0:T(8,128)}, u32[]{:S(2)}) copy-start(f32[6,64,512]{2,1,0:T(8,128)} %get-tuple-element.18) | copy-start | bytes 2359300
